TPU v7x, 512 devices: a whole 4x8x8 slice. The times are simulated.
512 devices in a mesh: row: 16 (over z, core), col: 32 (over y, x).
Axes of the slice: x: 4, y: 8, z: 8, core: 2. Of those that a mesh axis runs over, the one named last changes fastest.
Arguments:
- weight: float32 [3584, 18432], P('row', 'col'), may hold values from -6 to 6
- momentum: float32 [3584, 18432], P('row', 'col'), may hold values from -6 to 6
- gradients: float32 [2, 3584, 18432], P(None, 'row', 'col'), may hold values from -6 to 6
- basis: float32 [18432, 256], P('col'), may hold values from -6 to 6
- step: int32 [1], replicated, may hold values from 0 to 63
Outputs:
- new_weight: float32 [3584, 18432], P('row', 'col')
- new_momentum: float32 [3584, 18432], P('row', 'col')
- new_basis: float32 [18432, 256], P('col')
All inputs are finite; a program needn't handle non-finite values.
Results may differ from a plain program's by a relative error of at most 0.0004.
Values sent between devices are 32-bit elements; how exact they have to be, the bound alone decides.
A program may use at most 64 MiB of HBM per device.

v0:
```python
import functools

import jax
import jax.numpy as jnp
from jax import lax
from jax.experimental import pallas as pl
from jax.experimental.pallas import tpu as pltpu
from jax.sharding import PartitionSpec as P

F32 = jnp.float32
BF16 = jnp.bfloat16
LANES = 128
PIVOTS = 32
NN = (((1,), (0,)), ((), ()))
NT = (((1,), (1,)), ((), ()))
TN = (((0,), (0,)), ((), ()))


def exact(left, right, dims):
    return lax.dot_general(left, right, dims, precision=lax.Precision.HIGHEST, preferred_element_type=F32)


def split(value):
    high = value.astype(BF16)
    return high, (value - high.astype(F32)).astype(BF16)


def product(left, right, dims):
    def dot(a, b):
        return lax.dot_general(a, b, dims, preferred_element_type=F32)

    return dot(left[0], right[0]) + (dot(left[0], right[1]) + dot(left[1], right[0]))


def eliminate(table, phase):
    rank = table.shape[0]
    tiles = PIVOTS // 8
    base = phase * LANES
    live = [base + k * LANES for k in range(3)]
    rows = lax.broadcasted_iota(jnp.int32, (8, LANES), 0)
    lanes = lax.broadcasted_iota(jnp.int32, (PIVOTS, LANES), 1)

    def block(index, carry):
        offset = pl.multiple_of(index * PIVOTS, PIVOTS)
        start = pl.multiple_of(base + offset, PIVOTS)
        corner = table[pl.ds(start, PIVOTS), base : base + LANES]
        corner = pltpu.roll(corner, lax.rem(LANES - offset, LANES), 1)
        column = {}
        for j in range(PIVOTS):
            for t in range(j // 8, tiles):
                column[t, j] = jnp.broadcast_to(corner[8 * t : 8 * t + 8, j : j + 1], (8, LANES))
        part = {
            (t, i): table[pl.ds(start + 8 * t, 8), lane : lane + LANES] for t in range(tiles) for i, lane in enumerate(live)
        }
        for k in range(PIVOTS):
            top, at = k // 8, k % 8
            inverse = lax.rsqrt(column[top, k][at : at + 1, :])
            scaled = [column[t, k] * inverse if t >= top else None for t in range(tiles)]
            below = list(scaled)
            below[top] = jnp.where(rows > at, scaled[top], 0.0)
            for j in range(k + 1, PIVOTS):
                weight = scaled[j // 8][j % 8 : j % 8 + 1, :]
                for t in range(j // 8, tiles):
                    column[t, j] = column[t, j] - below[t] * weight
            for i in range(len(live)):
                own = part[top, i][at : at + 1, :] * inverse
                for t in range(top, tiles):
                    part[t, i] = part[t, i] - below[t] * own
                part[top, i] = jnp.where(rows == at, own, part[top, i])
        strips = [jnp.concatenate([part[t, i] for t in range(tiles)], axis=0) for i in range(len(live))]
        for i, lane in enumerate(live):
            table[pl.ds(start, PIVOTS), lane : lane + LANES] = strips[i]
        for r in range(phase, rank // LANES):
            left = strips[r - phase]
            if r == phase:
                left = jnp.where(lanes >= offset + PIVOTS, left, 0.0)
            first = 0 if r == phase else 1
            change = exact(left, jnp.concatenate(strips[first:], axis=1), TN)
            region = (slice(r * LANES, (r + 1) * LANES), slice(live[first], live[-1] + LANES))
            table[region] = table[region] - change
        return carry

    lax.fori_loop(0, LANES // PIVOTS, block, 0)


def kernel(
    din, n_row, n_col, weight, momentum, gradients, basis, step, weight_out, momentum_out, basis_out,
    w, m, g, v, b, partial, panel_in, panel, gram, gram_in, gram_all, table, ortho,
    h_part, h_in, h_sum, h_rows, h_all, f, squares, load_sem, send_sem, recv_sem,
):
    row, col = lax.axis_index("row"), lax.axis_index("col")
    core, z = lax.rem(row, 2), row // 2
    n_z = n_row // 2
    n_rows, n_cols = m.shape
    rank = v.shape[1]
    owned = panel_in.shape[2]
    owners = n_rows // owned
    strip = rank // n_col
    piece = n_cols // n_z
    half = rank // 2

    def on_col(other):
        return {"row": row, "col": other}

    def on_row(other):
        return {"row": other, "col": col}

    barrier = pltpu.get_barrier_semaphore()

    def greet_col(i, carry):
        pl.semaphore_signal(barrier, inc=1, device_id=on_col(lax.rem(col + i, n_col)))
        return carry

    def greet_row(i, carry):
        pl.semaphore_signal(barrier, inc=1, device_id=on_row(lax.rem(row + i, n_row)))
        return carry

    loads = [
        pltpu.make_async_copy(momentum, m, load_sem.at[0]),
        pltpu.make_async_copy(gradients, g, load_sem.at[1]),
        pltpu.make_async_copy(basis, v, load_sem.at[2]),
        pltpu.make_async_copy(weight, w, load_sem.at[3]),
    ]
    for load in loads:
        load.start()
    lax.fori_loop(1, n_col, greet_col, 0)
    lax.fori_loop(1, n_row, greet_row, 0)

    def remote(source, target, phase, s, device):
        return pltpu.make_async_remote_copy(
            src_ref=source, dst_ref=target, send_sem=send_sem.at[s, phase], recv_sem=recv_sem.at[s, phase],
            device_id=device, device_id_type=pl.DeviceIdType.MESH,
        )

    def arrived(block, phase, s):
        remote(block, block, phase, s, on_row(row + 1 - 2 * core)).wait_recv()

    def sent(block, phase, s):
        remote(block, block, phase, s, on_row(row + 1 - 2 * core)).wait_send()

    def to_cols(start):
        def body(i, carry):
            start(lax.rem(col + i, n_col))
            return carry

        lax.fori_loop(1, n_col, body, 0)

    def to_rows(start):
        def body(i, carry):
            start(lax.rem(row + i, n_row))
            return carry

        lax.fori_loop(1, n_row, body, 0)

    def to_layers(start):
        def body(i, carry):
            start(lax.rem(z + i, n_z))
            return carry

        lax.fori_loop(1, n_z, body, 0)

    for load in loads[:3]:
        load.wait()
    b[...] = m[...] + g[0]
    blocks = [(r, min(n_rows, r + 112)) for r in range(0, n_rows, 112)]
    start = split(v[...])
    for low, high in blocks:
        partial[0, low:high, :] = product(split(b[low:high, :]), start, NN)
    pl.semaphore_wait(barrier, n_col + n_row - 2)

    def panel_send(s):
        def start(other):
            @pl.when(other < owners)
            def _():
                remote(
                    partial.at[s, pl.ds(pl.multiple_of(other * owned, owned), owned)],
                    panel_in.at[s, col], 0, s, on_col(other),
                ).start()

        to_cols(start)

    def panel_finish(s):
        @pl.when(col < owners)
        def _():
            mine = pl.ds(pl.multiple_of(col * owned, owned), owned)
            panel_in[s, col] = partial[s, mine, :]
            arrived(panel_in.at[s, pl.ds(0, n_col - 1)], 0, s)
            panel[s, mine, :] = jnp.sum(panel_in[s], axis=0)

            def start(other):
                remote(panel.at[s, mine], panel.at[s, mine], 1, s, on_col(other)).start()

            to_cols(start)
            arrived(panel.at[s, pl.ds(0, (owners - 1) * owned)], 1, s)

        @pl.when(col >= owners)
        def _():
            arrived(panel.at[s], 1, s)

    def squares_send(s):
        squares[s, col] = jnp.sum(f[s] * f[s], axis=0, keepdims=True)

        def start(other):
            remote(squares.at[s, col], squares.at[s, col], 7, s, on_col(other)).start()

        to_cols(start)

    def scale_of(s):
        arrived(squares.at[s, pl.ds(0, n_col - 1)], 7, s)
        total = jnp.sum(squares[s], axis=0)
        return jnp.sqrt(total * (1.0 / din) + 1e-6)

    def weight_step(s, scale):
        rate = 0.5 * jnp.minimum(1.0, (step[0] + (s + 1)).astype(F32) / 64.0) * (n_rows * n_row / rank) ** 0.5
        right = split(f[s])
        for low, high in blocks:
            left = split(ortho[s, low:high, :] * (rate / scale))
            w[low:high, :] = w[low:high, :] - product(left, right, NT)

    panel_send(0)
    for s in range(2):
        if s == 1:
            squares_send(0)
            loads[3].wait()
            weight_step(0, scale_of(0))
        panel_finish(s)

        gram[s] = exact(panel[s], panel[s], TN)
        strip_here = pl.ds(pl.multiple_of(col * strip, strip), strip)

        def gram_send(other, s=s):
            remote(gram.at[s, strip_here], gram_in.at[s, row], 2, s, on_row(other)).start()

        to_rows(gram_send)
        gram_in[s, row] = gram[s, strip_here, :]

        panel_parts = split(panel[s])
        for low in range(0, n_cols, LANES):
            high = min(n_cols, low + LANES)
            part = product(split(b[:, low:high]), panel_parts, TN)
            for k in range(2):
                h_part[s, k, low:high, :] = part[:, k * half : (k + 1) * half]
        remote(h_part.at[s, 1 - core], h_in.at[s], 4, s, on_row(row + 1 - 2 * core)).start()

        def piece_of(other):
            return pl.ds(pl.multiple_of(other * piece, 8), piece)

        def h_send(other, s=s):
            remote(h_sum.at[s, piece_of(other)], h_rows.at[s, z], 5, s, on_row(2 * other + core)).start()

        def h_share(other, s=s):
            mine = h_all.at[s, core, piece_of(z)]
            remote(mine, mine, 6, s, on_row(2 * other + core)).start()

        upper = col < n_col // 2
        right = pl.ds(half, half)

        def gram_share(other, s=s):
            @pl.when(upper)
            def _():
                remote(gram_all.at[s, strip_here], gram_all.at[s, strip_here], 3, s, on_col(other)).start()

            @pl.when(jnp.logical_not(upper))
            def _():
                mine = gram_all.at[s, strip_here, right]
                remote(mine, mine, 9, s, on_col(other)).start()

        arrived(h_in.at[s], 4, s)
        h_sum[s] = h_part[s, core] + h_in[s]
        to_layers(h_send)
        h_rows[s, z] = h_sum[s, piece_of(z), :]

        arrived(gram_in.at[s, pl.ds(0, n_row - 1)], 2, s)
        gram_all[s, strip_here, :] = jnp.sum(gram_in[s], axis=0)
        to_cols(gram_share)

        table[:, rank:] = jnp.where(
            lax.broadcasted_iota(jnp.int32, (rank, rank), 0) == lax.broadcasted_iota(jnp.int32, (rank, rank), 1), 1.0, 0.0
        )
        arrived(h_rows.at[s, pl.ds(0, n_z - 1)], 5, s)
        h_all[s, core, piece_of(z), :] = jnp.sum(h_rows[s], axis=0)
        to_layers(h_share)

        @pl.when(upper)
        def _(s=s):
            arrived(gram_all.at[s, pl.ds(0, half - strip)], 3, s)
            arrived(gram_all.at[s, pl.ds(0, half), right], 9, s)

        @pl.when(jnp.logical_not(upper))
        def _(s=s):
            arrived(gram_all.at[s, pl.ds(0, half)], 3, s)
            arrived(gram_all.at[s, pl.ds(0, half - strip), right], 9, s)

        table[:half, :rank] = gram_all[s, :half, :]
        table[half:, half:rank] = gram_all[s, half:, half:]
        eliminate(table, 0)
        eliminate(table, 1)
        arrived(h_all.at[s, 0, pl.ds(0, n_cols - piece)], 6, s)
        remote(h_all.at[s, core], h_all.at[s, core], 8, s, on_row(row + 1 - 2 * core)).start()

        inverse = split(table[:, rank:])
        for low, high in blocks:
            ortho[s, low:high, :] = product(split(panel[s, low:high, :]), inverse, NT)
        arrived(h_all.at[s, 0], 8, s)
        for low in range(0, n_cols, 192):
            high = min(n_cols, low + 192)
            f[s, low:high, :] = sum(
                product(split(h_all[s, k, low:high, :]), [x[:, k * half : (k + 1) * half] for x in inverse], NT) for k in range(2)
            )
        if s == 1:
            squares_send(1)
        right = split(f[s])
        for low, high in blocks:
            b[low:high, :] = b[low:high, :] - 0.05 * product(split(ortho[s, low:high, :]), right, NT)
            if s == 0:
                b[low:high, :] = b[low:high, :] + g[1, low:high, :]
                partial[1, low:high, :] = product(split(b[low:high, :]), right, NN)
        if s == 0:
            panel_send(1)

    momentum_out[...] = b[...]
    scale = scale_of(1)
    basis_out[...] = f[1] / scale
    weight_step(1, scale)
    weight_out[...] = w[...]

    for s in range(2):
        @pl.when(col < owners)
        def _(s=s):
            sent(panel_in.at[s, pl.ds(0, owners - 1)], 0, s)
            sent(panel_in.at[s, pl.ds(0, n_col - 1)], 1, s)

        @pl.when(col >= owners)
        def _(s=s):
            sent(panel_in.at[s, pl.ds(0, owners)], 0, s)

        sent(gram_in.at[s, pl.ds(0, n_row - 1)], 2, s)

        @pl.when(col < n_col // 2)
        def _(s=s):
            sent(gram_all.at[s, pl.ds(0, (n_col - 1) * strip)], 3, s)

        @pl.when(col >= n_col // 2)
        def _(s=s):
            sent(gram_all.at[s, pl.ds(0, (n_col - 1) * strip), pl.ds(half, half)], 9, s)

        sent(h_in.at[s], 4, s)
        sent(h_rows.at[s, pl.ds(0, n_z - 1)], 5, s)
        sent(h_rows.at[s, pl.ds(0, n_z - 1)], 6, s)
        sent(squares.at[s, pl.ds(0, n_col - 1)], 7, s)
        sent(h_in.at[s], 8, s)


def solution(mesh):
    n_row, n_col = mesh.shape["row"], mesh.shape["col"]

    def local(weight, momentum, gradients, basis, step):
        (n_rows, n_cols), rank = weight.shape, basis.shape[1]
        owned = -(-n_rows // (8 * n_col)) * 8
        anywhere = pl.BlockSpec(memory_space=pltpu.HBM)
        vmem = functools.partial(pltpu.VMEM, dtype=F32)
        half, n_z = rank // 2, n_row // 2
        return pl.pallas_call(
            functools.partial(kernel, n_cols * n_col, n_row, n_col),
            out_shape=(
                jax.ShapeDtypeStruct(weight.shape, F32),
                jax.ShapeDtypeStruct(weight.shape, F32),
                jax.ShapeDtypeStruct(basis.shape, F32),
            ),
            in_specs=[anywhere] * 4 + [pl.BlockSpec(memory_space=pltpu.SMEM)],
            out_specs=(pl.BlockSpec(memory_space=pltpu.VMEM),) * 3,
            scratch_shapes=[
                vmem((n_rows, n_cols)),
                vmem((n_rows, n_cols)),
                vmem((2, n_rows, n_cols)),
                vmem((n_cols, rank)),
                vmem((n_rows, n_cols)),
                vmem((2, n_rows, rank)),
                vmem((2, n_col, owned, rank)),
                vmem((2, n_rows, rank)),
                vmem((2, rank, rank)),
                vmem((2, n_row, rank // n_col, rank)),
                vmem((2, rank, rank)),
                vmem((rank, 2 * rank)),
                vmem((2, n_rows, rank)),
                vmem((2, 2, n_cols, half)),
                vmem((2, n_cols, half)),
                vmem((2, n_cols, half)),
                vmem((2, n_z, n_cols // n_z, half)),
                vmem((2, 2, n_cols, half)),
                vmem((2, n_cols, rank)),
                vmem((2, n_col, 1, rank)),
                pltpu.SemaphoreType.DMA((4,)),
                pltpu.SemaphoreType.DMA((2, 10)),
                pltpu.SemaphoreType.DMA((2, 10)),
            ],
            compiler_params=pltpu.CompilerParams(collective_id=0, has_side_effects=True, vmem_limit_bytes=54500 * 1024),
        )(weight, momentum, gradients, basis, step)

    return jax.shard_map(
        local,
        mesh=mesh,
        in_specs=(P("row", "col"), P("row", "col"), P(None, "row", "col"), P("col", None), P()),
        out_specs=(P("row", "col"), P("row", "col"), P("col", None)),
        check_vma=False,
    )
```

profile of v0, /device:TPU:1, one launch (start us, length us, event | category | flops | bytes accessed | tf_op | source)
XLA Modules:
  0.0 122.2 jit_solution(2915925866070619541)
XLA Ops:
  1.3 118.0 %shard_map.76 = (f32[224,576]{1,0:T(8,128)S(1)}, f32[224,576]{1,0:T(8,128)}, f32[576,256]{1,0:T(8,128)}) custom-call(f32[224,576]{1,0:T(8,128)} %weight.1, f32[224,576]{1,0:T(8,128)} %momentum.1, f32[2,224,576]{2,1,0:T(8,128)} %gradients.1, f32[576,256]{1,0:T(8,128)} %basis.1, s32[1]{0:T(128)S(6)} %copy.11.step), custom_call_target="tpu_custom_call" | custom-call | tf_op jit(solution)/shard_map/pallas_call | solution.py:363
  119.3 0.0 copy-start.1
  119.3 0.0 copy-start
  119.3 0.8 copy.12
  120.1 0.4 copy-done.1
  120.6 0.8 copy.13
  121.4 0.0 copy-done
  121.4 0.8 copy.14
Async XLA Ops:
  119.3 1.3 %copy-start.1 = (f32[224,576]{1,0:T(8,128)S(1)}, f32[224,576]{1,0:T(8,128)}, u32[]{:S(2)}) copy-start(f32[224,576]{1,0:T(8,128)} %get-tuple-element.7) | copy-start | bytes 1548292
  119.3 2.1 %copy-start = (f32[576,256]{1,0:T(8,128)S(1)}, f32[576,256]{1,0:T(8,128)}, u32[]{:S(2)}) copy-start(f32[576,256]{1,0:T(8,128)} %get-tuple-element.8) | copy-start | bytes 1769476
where the time goes:
time: 122 us
  Pallas kernels  118 us (97%)
  local copies, waits for them, and re-layouts  2.88 us (2%)
  between operations  1.3 us (1%)
    pallas_call x1, Pallas kernels, local(): pl.pallas_call(functools.partial(kernel, n_cols * n_col, n_row, n_col), o...  118 us
    unnamed x7, local copies, waits for them, and re-layouts  2.88 us

commit v1 on v0

--- a/solution.py
+++ b/solution.py
@@ -32,6 +32,22 @@
     return dot(left[0], right[0]) + (dot(left[0], right[1]) + dot(left[1], right[0]))
 
 
+def stacked(left, right):
+    def thirds(value):
+        high, rest = value.astype(BF16), value - value.astype(BF16).astype(F32)
+        middle = rest.astype(BF16)
+        return high, middle, (rest - middle.astype(F32)).astype(BF16)
+
+    a, b = thirds(left), thirds(right)
+    pairs = ((0, 2), (2, 0), (1, 1), (0, 1), (1, 0), (0, 0))
+    return lax.dot_general(
+        jnp.concatenate([a[i] for i, _ in pairs], axis=0),
+        jnp.concatenate([b[j] for _, j in pairs], axis=0),
+        TN,
+        preferred_element_type=F32,
+    )
+
+
 def eliminate(table, phase):
     rank = table.shape[0]
     tiles = PIVOTS // 8
@@ -44,11 +60,12 @@
         offset = pl.multiple_of(index * PIVOTS, PIVOTS)
         start = pl.multiple_of(base + offset, PIVOTS)
         corner = table[pl.ds(start, PIVOTS), base : base + LANES]
-        corner = pltpu.roll(corner, lax.rem(LANES - offset, LANES), 1)
         column = {}
         for j in range(PIVOTS):
             for t in range(j // 8, tiles):
-                column[t, j] = jnp.broadcast_to(corner[8 * t : 8 * t + 8, j : j + 1], (8, LANES))
+                column[t, j] = jnp.take_along_axis(
+                    corner[8 * t : 8 * t + 8, :], jnp.full((8, LANES), offset + j, jnp.int32), axis=1, mode="promise_in_bounds"
+                )
         part = {
             (t, i): table[pl.ds(start + 8 * t, 8), lane : lane + LANES] for t in range(tiles) for i, lane in enumerate(live)
         }
@@ -75,7 +92,7 @@
             if r == phase:
                 left = jnp.where(lanes >= offset + PIVOTS, left, 0.0)
             first = 0 if r == phase else 1
-            change = exact(left, jnp.concatenate(strips[first:], axis=1), TN)
+            change = stacked(left, jnp.concatenate(strips[first:], axis=1))
             region = (slice(r * LANES, (r + 1) * LANES), slice(live[first], live[-1] + LANES))
             table[region] = table[region] - change
         return carry
@@ -105,26 +122,30 @@
     def on_row(other):
         return {"row": other, "col": col}
 
+    def others(me, count, act):
+        for i in range(count - 1):
+            away = count // 2 + ((i + 1) // 2) * (1 - 2 * (i % 2))
+            act(jnp.where(me + away >= count, me + (away - count), me + away))
+
     barrier = pltpu.get_barrier_semaphore()
 
-    def greet_col(i, carry):
-        pl.semaphore_signal(barrier, inc=1, device_id=on_col(lax.rem(col + i, n_col)))
-        return carry
-
-    def greet_row(i, carry):
-        pl.semaphore_signal(barrier, inc=1, device_id=on_row(lax.rem(row + i, n_row)))
-        return carry
+    def greet_col(other):
+        pl.semaphore_signal(barrier, inc=1, device_id=on_col(other))
+
+    def greet_row(other):
+        pl.semaphore_signal(barrier, inc=1, device_id=on_row(other))
 
     loads = [
         pltpu.make_async_copy(momentum, m, load_sem.at[0]),
-        pltpu.make_async_copy(gradients, g, load_sem.at[1]),
+        pltpu.make_async_copy(gradients.at[0], g.at[0], load_sem.at[1]),
         pltpu.make_async_copy(basis, v, load_sem.at[2]),
         pltpu.make_async_copy(weight, w, load_sem.at[3]),
+        pltpu.make_async_copy(gradients.at[1], g.at[1], load_sem.at[4]),
     ]
-    for load in loads:
+    for load in loads[:3]:
         load.start()
-    lax.fori_loop(1, n_col, greet_col, 0)
-    lax.fori_loop(1, n_row, greet_row, 0)
+    others(col, n_col, greet_col)
+    others(row, n_row, greet_row)
 
     def remote(source, target, phase, s, device):
         return pltpu.make_async_remote_copy(
@@ -138,29 +159,10 @@
     def sent(block, phase, s):
         remote(block, block, phase, s, on_row(row + 1 - 2 * core)).wait_send()
 
-    def to_cols(start):
-        def body(i, carry):
-            start(lax.rem(col + i, n_col))
-            return carry
-
-        lax.fori_loop(1, n_col, body, 0)
-
-    def to_rows(start):
-        def body(i, carry):
-            start(lax.rem(row + i, n_row))
-            return carry
-
-        lax.fori_loop(1, n_row, body, 0)
-
-    def to_layers(start):
-        def body(i, carry):
-            start(lax.rem(z + i, n_z))
-            return carry
-
-        lax.fori_loop(1, n_z, body, 0)
-
     for load in loads[:3]:
         load.wait()
+    for load in loads[3:]:
+        load.start()
     b[...] = m[...] + g[0]
     blocks = [(r, min(n_rows, r + 112)) for r in range(0, n_rows, 112)]
     start = split(v[...])
@@ -168,34 +170,47 @@
         partial[0, low:high, :] = product(split(b[low:high, :]), start, NN)
     pl.semaphore_wait(barrier, n_col + n_row - 2)
 
+    sides = [pl.ds(k * half, half) for k in range(2)]
+    panel_phases = ((0, 1), (11, 12))
+
     def panel_send(s):
-        def start(other):
-            @pl.when(other < owners)
-            def _():
-                remote(
-                    partial.at[s, pl.ds(pl.multiple_of(other * owned, owned), owned)],
-                    panel_in.at[s, col], 0, s, on_col(other),
-                ).start()
-
-        to_cols(start)
-
-    def panel_finish(s):
+        for side, (phase, _) in zip(sides, panel_phases):
+
+            def start(other, side=side, phase=phase):
+                @pl.when(other < owners)
+                def _():
+                    remote(
+                        partial.at[s, pl.ds(pl.multiple_of(other * owned, owned), owned), side],
+                        panel_in.at[s, col, :, side], phase, s, on_col(other),
+                    ).start()
+
+            others(col, n_col, start)
+
+    def panel_finish(s, meanwhile):
         @pl.when(col < owners)
         def _():
             mine = pl.ds(pl.multiple_of(col * owned, owned), owned)
             panel_in[s, col] = partial[s, mine, :]
-            arrived(panel_in.at[s, pl.ds(0, n_col - 1)], 0, s)
-            panel[s, mine, :] = jnp.sum(panel_in[s], axis=0)
-
-            def start(other):
-                remote(panel.at[s, mine], panel.at[s, mine], 1, s, on_col(other)).start()
-
-            to_cols(start)
-            arrived(panel.at[s, pl.ds(0, (owners - 1) * owned)], 1, s)
-
-        @pl.when(col >= owners)
-        def _():
-            arrived(panel.at[s], 1, s)
+            for side, (arrival, spread) in zip(sides, panel_phases):
+                arrived(panel_in.at[s, pl.ds(0, n_col - 1), :, side], arrival, s)
+                panel[s, mine, side] = jnp.sum(panel_in[s, :, :, side], axis=0)
+
+                def start(other, side=side, spread=spread):
+                    block = panel.at[s, mine, side]
+                    remote(block, block, spread, s, on_col(other)).start()
+
+                others(col, n_col, start)
+
+        meanwhile()
+        for side, (_, spread) in zip(sides, panel_phases):
+
+            @pl.when(col < owners)
+            def _(side=side, spread=spread):
+                arrived(panel.at[s, pl.ds(0, (owners - 1) * owned), side], spread, s)
+
+            @pl.when(col >= owners)
+            def _(side=side, spread=spread):
+                arrived(panel.at[s, :, side], spread, s)
 
     def squares_send(s):
         squares[s, col] = jnp.sum(f[s] * f[s], axis=0, keepdims=True)
@@ -203,35 +218,51 @@
         def start(other):
             remote(squares.at[s, col], squares.at[s, col], 7, s, on_col(other)).start()
 
-        to_cols(start)
+        others(col, n_col, start)
 
     def scale_of(s):
         arrived(squares.at[s, pl.ds(0, n_col - 1)], 7, s)
         total = jnp.sum(squares[s], axis=0)
-        return jnp.sqrt(total * (1.0 / din) + 1e-6)
-
-    def weight_step(s, scale):
+        return 1.0 / jnp.sqrt(total * (1.0 / din) + 1e-6)
+
+    def weight_step(target, s, scale, right):
         rate = 0.5 * jnp.minimum(1.0, (step[0] + (s + 1)).astype(F32) / 64.0) * (n_rows * n_row / rank) ** 0.5
-        right = split(f[s])
         for low, high in blocks:
-            left = split(ortho[s, low:high, :] * (rate / scale))
-            w[low:high, :] = w[low:high, :] - product(left, right, NT)
+            left = split(ortho[s, low:high, :] * (rate * scale))
+            target[low:high, :] = w[low:high, :] - product(left, right, NT)
 
     panel_send(0)
     for s in range(2):
         if s == 1:
             squares_send(0)
-            loads[3].wait()
-            weight_step(0, scale_of(0))
-        panel_finish(s)
+
+        def meanwhile(s=s):
+            if s == 1:
+                weight_step(w, 0, scale_of(0), split(f[0]))
+            else:
+                for load in loads[3:]:
+                    load.wait()
+
+        panel_finish(s, meanwhile)
 
         gram[s] = exact(panel[s], panel[s], TN)
         strip_here = pl.ds(pl.multiple_of(col * strip, strip), strip)
 
+        upper = col < n_col // 2
+        left, right = sides
+
         def gram_send(other, s=s):
-            remote(gram.at[s, strip_here], gram_in.at[s, row], 2, s, on_row(other)).start()
-
-        to_rows(gram_send)
+            remote(gram.at[s, strip_here, right], gram_in.at[s, row, :, right], 2, s, on_row(other)).start()
+
+        def gram_send_left(other, s=s):
+            remote(gram.at[s, strip_here, left], gram_in.at[s, row, :, left], 10, s, on_row(other)).start()
+
+        others(row, n_row, gram_send)
+
+        @pl.when(upper)
+        def _():
+            others(row, n_row, gram_send_left)
+
         gram_in[s, row] = gram[s, strip_here, :]
 
         panel_parts = split(panel[s])
@@ -252,44 +283,45 @@
             mine = h_all.at[s, core, piece_of(z)]
             remote(mine, mine, 6, s, on_row(2 * other + core)).start()
 
-        upper = col < n_col // 2
-        right = pl.ds(half, half)
-
         def gram_share(other, s=s):
-            @pl.when(upper)
-            def _():
-                remote(gram_all.at[s, strip_here], gram_all.at[s, strip_here], 3, s, on_col(other)).start()
-
-            @pl.when(jnp.logical_not(upper))
-            def _():
-                mine = gram_all.at[s, strip_here, right]
-                remote(mine, mine, 9, s, on_col(other)).start()
+            block = gram_all.at[s, strip_here, right]
+            remote(block, block, 9, s, on_col(other)).start()
+
+        def gram_share_left(other, s=s):
+            block = gram_all.at[s, strip_here, left]
+            remote(block, block, 3, s, on_col(other)).start()
 
         arrived(h_in.at[s], 4, s)
         h_sum[s] = h_part[s, core] + h_in[s]
-        to_layers(h_send)
+        others(z, n_z, h_send)
         h_rows[s, z] = h_sum[s, piece_of(z), :]
 
-        arrived(gram_in.at[s, pl.ds(0, n_row - 1)], 2, s)
-        gram_all[s, strip_here, :] = jnp.sum(gram_in[s], axis=0)
-        to_cols(gram_share)
+        arrived(gram_in.at[s, pl.ds(0, n_row - 1), :, right], 2, s)
+        gram_all[s, strip_here, right] = jnp.sum(gram_in[s, :, :, right], axis=0)
+        others(col, n_col, gram_share)
+
+        @pl.when(upper)
+        def _(s=s):
+            arrived(gram_in.at[s, pl.ds(0, n_row - 1), :, left], 10, s)
+            gram_all[s, strip_here, left] = jnp.sum(gram_in[s, :, :, left], axis=0)
+            others(col, n_col, gram_share_left)
 
         table[:, rank:] = jnp.where(
             lax.broadcasted_iota(jnp.int32, (rank, rank), 0) == lax.broadcasted_iota(jnp.int32, (rank, rank), 1), 1.0, 0.0
         )
         arrived(h_rows.at[s, pl.ds(0, n_z - 1)], 5, s)
         h_all[s, core, piece_of(z), :] = jnp.sum(h_rows[s], axis=0)
-        to_layers(h_share)
+        others(z, n_z, h_share)
+
+        arrived(gram_all.at[s, pl.ds(0, rank - strip), right], 9, s)
 
         @pl.when(upper)
         def _(s=s):
-            arrived(gram_all.at[s, pl.ds(0, half - strip)], 3, s)
-            arrived(gram_all.at[s, pl.ds(0, half), right], 9, s)
+            arrived(gram_all.at[s, pl.ds(0, half - strip), left], 3, s)
 
         @pl.when(jnp.logical_not(upper))
         def _(s=s):
-            arrived(gram_all.at[s, pl.ds(0, half)], 3, s)
-            arrived(gram_all.at[s, pl.ds(0, half - strip), right], 9, s)
+            arrived(gram_all.at[s, pl.ds(0, half), left], 3, s)
 
         table[:half, :rank] = gram_all[s, :half, :]
         table[half:, half:rank] = gram_all[s, half:, half:]
@@ -301,12 +333,23 @@
         inverse = split(table[:, rank:])
         for low, high in blocks:
             ortho[s, low:high, :] = product(split(panel[s, low:high, :]), inverse, NT)
+        thirds = [(low, min(n_cols, low + 192)) for low in range(0, n_cols, 192)]
+
+        def factor_half(k, low, high, s=s):
+            side = split(table[:, pl.ds(pl.multiple_of(rank + k * half, LANES), half)])
+            rows = split(h_all[s, k, low:high, :])
+            return lax.dot_general(
+                jnp.concatenate([rows[0], rows[1], rows[0]], axis=1),
+                jnp.concatenate([side[1], side[0], side[0]], axis=1),
+                NT,
+                preferred_element_type=F32,
+            )
+
+        for low, high in thirds:
+            f[s, low:high, :] = factor_half(core, low, high)
         arrived(h_all.at[s, 0], 8, s)
-        for low in range(0, n_cols, 192):
-            high = min(n_cols, low + 192)
-            f[s, low:high, :] = sum(
-                product(split(h_all[s, k, low:high, :]), [x[:, k * half : (k + 1) * half] for x in inverse], NT) for k in range(2)
-            )
+        for low, high in thirds:
+            f[s, low:high, :] = f[s, low:high, :] + factor_half(1 - core, low, high)
         if s == 1:
             squares_send(1)
         right = split(f[s])
@@ -320,29 +363,28 @@
 
     momentum_out[...] = b[...]
     scale = scale_of(1)
-    basis_out[...] = f[1] / scale
-    weight_step(1, scale)
-    weight_out[...] = w[...]
+    weight_step(weight_out, 1, scale, right)
+    basis_out[...] = f[1] * scale
 
     for s in range(2):
-        @pl.when(col < owners)
-        def _(s=s):
-            sent(panel_in.at[s, pl.ds(0, owners - 1)], 0, s)
-            sent(panel_in.at[s, pl.ds(0, n_col - 1)], 1, s)
-
-        @pl.when(col >= owners)
-        def _(s=s):
-            sent(panel_in.at[s, pl.ds(0, owners)], 0, s)
-
-        sent(gram_in.at[s, pl.ds(0, n_row - 1)], 2, s)
+        for side, (arrival, spread) in zip(sides, panel_phases):
+
+            @pl.when(col < owners)
+            def _(s=s, side=side, arrival=arrival, spread=spread):
+                sent(panel_in.at[s, pl.ds(0, owners - 1), :, side], arrival, s)
+                sent(panel_in.at[s, pl.ds(0, n_col - 1), :, side], spread, s)
+
+            @pl.when(col >= owners)
+            def _(s=s, side=side, arrival=arrival):
+                sent(panel_in.at[s, pl.ds(0, owners), :, side], arrival, s)
+
+        sent(gram_in.at[s, pl.ds(0, n_row - 1), :, sides[1]], 2, s)
+        sent(gram_all.at[s, pl.ds(0, (n_col - 1) * strip), sides[1]], 9, s)
 
         @pl.when(col < n_col // 2)
         def _(s=s):
-            sent(gram_all.at[s, pl.ds(0, (n_col - 1) * strip)], 3, s)
-
-        @pl.when(col >= n_col // 2)
-        def _(s=s):
-            sent(gram_all.at[s, pl.ds(0, (n_col - 1) * strip), pl.ds(half, half)], 9, s)
+            sent(gram_in.at[s, pl.ds(0, n_row - 1), :, sides[0]], 10, s)
+            sent(gram_all.at[s, pl.ds(0, (n_col - 1) * strip), sides[0]], 3, s)
 
         sent(h_in.at[s], 4, s)
         sent(h_rows.at[s, pl.ds(0, n_z - 1)], 5, s)
@@ -390,9 +432,9 @@
                 vmem((2, 2, n_cols, half)),
                 vmem((2, n_cols, rank)),
                 vmem((2, n_col, 1, rank)),
-                pltpu.SemaphoreType.DMA((4,)),
-                pltpu.SemaphoreType.DMA((2, 10)),
-                pltpu.SemaphoreType.DMA((2, 10)),
+                pltpu.SemaphoreType.DMA((5,)),
+                pltpu.SemaphoreType.DMA((2, 13)),
+                pltpu.SemaphoreType.DMA((2, 13)),
             ],
             compiler_params=pltpu.CompilerParams(collective_id=0, has_side_effects=True, vmem_limit_bytes=54500 * 1024),
         )(weight, momentum, gradients, basis, step)

time: 122 us -> 109 us (0.89)
  Pallas kernels: 118 us -> 104 us
    pallas_call x1, Pallas kernels: 118 us -> 104 us  [local(): pl.pallas_call(functools.partial(kernel, n_cols * n_col, n_row, n_col), o...]
where the time goes in v1:
time: 109 us; the launch traced here: 108 us
  Pallas kernels  104 us (95%)
  local copies, waits for them, and re-layouts  2.88 us (3%)
  between operations  1.3 us (1%)
    pallas_call x1, Pallas kernels, local(): pl.pallas_call(functools.partial(kernel, n_cols * n_col, n_row, n_col), o...  104 us
    unnamed x7, local copies, waits for them, and re-layouts  2.88 us

profile of v1, /device:TPU:1, one launch (start us, length us, event | category | flops | bytes accessed | tf_op | source)
XLA Modules:
  0.0 108.5 jit_solution(15131381905500197270)
XLA Ops:
  1.3 104.3 %shard_map.76 = (f32[224,576]{1,0:T(8,128)S(1)}, f32[224,576]{1,0:T(8,128)}, f32[576,256]{1,0:T(8,128)}) custom-call(f32[224,576]{1,0:T(8,128)} %weight.1, f32[224,576]{1,0:T(8,128)} %momentum.1, f32[2,224,576]{2,1,0:T(8,128)} %gradients.1, f32[576,256]{1,0:T(8,128)} %basis.1, s32[1]{0:T(128)S(6)} %copy.11.step), custom_call_target="tpu_custom_call" | custom-call | tf_op jit(solution)/shard_map/pallas_call | solution.py:405
  105.6 0.0 copy-start.1
  105.6 0.0 copy-start
  105.6 0.8 copy.12
  106.4 0.4 copy-done.1
  106.8 0.8 copy.13
  107.6 0.0 copy-done
  107.7 0.8 copy.14
Async XLA Ops:
  105.6 1.3 %copy-start.1 = (f32[224,576]{1,0:T(8,128)S(1)}, f32[224,576]{1,0:T(8,128)}, u32[]{:S(2)}) copy-start(f32[224,576]{1,0:T(8,128)} %get-tuple-element.7) | copy-start | bytes 1548292
  105.6 2.1 %copy-start = (f32[576,256]{1,0:T(8,128)S(1)}, f32[576,256]{1,0:T(8,128)}, u32[]{:S(2)}) copy-start(f32[576,256]{1,0:T(8,128)} %get-tuple-element.8) | copy-start | bytes 1769476
